TPU v7x, 32 devices: a whole 2x2x4 slice. The times are simulated.
32 devices in a mesh: dp: 4 (over y, x), vocab: 8 (over z, core).
Axes of the slice: x: 2, y: 2, z: 4, core: 2. Of those that a mesh axis runs over, the one named last changes fastest.
Arguments:
- hidden: bfloat16 [256, 3072], P(('dp', 'vocab')), parts along dimension 0, may hold values from -60 to 60
- weight: bfloat16 [3072, 8192], P(None, 'vocab'), may hold values from -0.32421875 to 0.32421875
- targets: int32 [256], P('dp'), parts along dimension 0, may hold values from 0 to 8191
Outputs:
- loss: float32 [4], P('dp'), parts along dimension 0
- d_hidden: bfloat16 [256, 3072], P(('dp', 'vocab')), parts along dimension 0
- d_weight: bfloat16 [12288, 8192], P('dp', 'vocab'), parts along dimension 0
There are 4 independent parts, one for each index of `dp`. A program takes and returns all parts, laid end to end along the dimension named above; an argument that names none is the same for every part. Nothing has to cross between parts.
All inputs are finite; a program needn't handle non-finite values.
Results may differ from a plain program's by a relative error of at most 0.0035.
Values may be sent and summed in bfloat16 or wider, within the bound.
A program may use at most 64 MiB of HBM per device.

v0:
```python
import jax
import jax.numpy as jnp
from jax import lax
from jax.sharding import PartitionSpec as P


def joined(value, axis, combine):
    everything = jax.tree.map(lambda part: lax.all_gather(part, axis), value)
    initial = jax.tree.map(lambda part: part[0], everything)

    def hop(k, so_far):
        return combine(so_far, jax.tree.map(lambda part: part[k], everything))

    return lax.fori_loop(1, lax.axis_size(axis), hop, initial)


def combine_stats(first, second):
    top = jnp.maximum(first[0], second[0])
    total = first[1] * jnp.exp(first[0] - top) + second[1] * jnp.exp(second[0] - top)
    return (top, total, first[2] + second[2])


def body(hidden, weight, targets):
    gathered = lax.all_gather(hidden, "vocab", axis=0, tiled=True)
    logits = jnp.dot(gathered, weight, preferred_element_type=jnp.float32)
    width = weight.shape[1]
    offset = lax.axis_index("vocab") * width
    columns = offset + lax.broadcasted_iota(jnp.int32, (1, width), 1)
    hits = columns == targets[:, None]
    picked_local = jnp.sum(jnp.where(hits, logits, jnp.zeros_like(logits)), axis=1)
    local_top = jnp.max(logits, axis=1)
    local_total = jnp.sum(jnp.exp(logits - local_top[:, None]), axis=1)
    top, total, picked = joined((local_top, local_total, picked_local), "vocab", combine_stats)
    loss = jnp.mean(top + jnp.log(total) - picked).reshape(1)
    grad_logits = (
        jnp.exp(logits - top[:, None]) / total[:, None] - hits.astype(jnp.float32)
    ).astype(jnp.bfloat16)
    d_weight = lax.dot_general(
        gathered, grad_logits, (((0,), (0,)), ((), ())), preferred_element_type=jnp.float32
    ).astype(jnp.bfloat16)
    own_rows = hidden.shape[0]
    partial_value = lax.dot_general(
        grad_logits, weight, (((1,), (1,)), ((), ())), preferred_element_type=jnp.float32
    )
    everything = lax.psum(partial_value, "vocab")
    summed = lax.dynamic_slice_in_dim(everything, lax.axis_index("vocab") * own_rows, own_rows, 0)
    return (loss, summed.astype(jnp.bfloat16), d_weight)


def solution(mesh):
    placed = (P(("dp", "vocab"), None), P(None, "vocab"), P("dp"))
    return jax.shard_map(
        body,
        mesh=mesh,
        in_specs=placed,
        out_specs=(P("dp"), P(("dp", "vocab"), None), P("dp", "vocab")),
        check_vma=False,
    )
```

profile of v0, /device:TPU:0, one launch (start us, length us, event | category | flops | bytes accessed | tf_op | source)
XLA Modules:
  0.0 96.6 jit_solution(8625070616558614490)
XLA Ops:
  0.6 0.0 copy-start
  0.6 1.2 %dynamic-slice = u32[1]{0:T(128)} dynamic-slice(u32[32]{0:T(128)} %constant.59, u32[]{:T(128)S(6)} %add.78), dynamic_slice_sizes={1} | dynamic-slice | bytes 12
  2.6 16.4 %all_gather.21 = bf16[64,3072]{1,0:T(8,128)(2,1)S(1)} all-gather(bf16[8,3072]{1,0:T(8,128)(2,1)} %param.5), channel_id=1, replica_groups=mesh['dp'=4,'vocab'=8] {'vocab'}, dimensions={0}, use_global_device_ids=true | all-gather | bytes 442368 | tf_op jit(solution)/shard_map/all_gather | solution.py:24
  19.0 4.1 %fusion.14 = (f32[64]{0:T(128)S(1)}, f32[64,1024]{1,0:T(8,128)S(1)}) fusion(bf16[64,3072]{1,0:T(8,128)(2,1)S(1)} %all_gather.21, bf16[3072,1024]{1,0:T(8,128)(2,1)} %param.6), kind=kOutput, calls=%fused_computation.21 | convolution fusion | flops 402718656 | bytes 6947072 | tf_op jit(solution)/shard_map/dot_general | solution.py:25
  23.1 0.2 dynamic-update-slice
  23.4 0.0 copy-done
  23.4 0.2 fusion.7
  23.6 0.2 dynamic-update-slice.2
  23.8 0.2 dynamic-update-slice.1
  24.0 17.2 %all-reduce.3 = (f32[512]{0:T(512)S(1)}, f32[512]{0:T(512)S(1)}, f32[512]{0:T(512)S(1)}) all-reduce(f32[512]{0:T(512)S(1)} %dynamic-update-slice, f32[512]{0:T(512)S(1)} %dynamic-update-slice.1, f32[512]{0:T(512)S(1)} %dynamic-update-slice.2), channel_id=2, replica_groups=mesh['dp'=4,'vocab'=8] {'vocab'}, use_global_device_ids=true, to_apply=%add | all-reduce | flops 1536 | bytes 12288
  41.2 0.1 reshape.21
  41.3 0.1 reshape.20
  41.4 0.1 reshape.19
  41.5 0.3 while.19
  41.8 0.6 subtract_reduce_fusion
  43.0 4.8 %fusion.11 = f32[64,3072]{1,0:T(8,128)S(1)} fusion(bf16[3072,1024]{1,0:T(8,128)(2,1)} %param.6, f32[64,1024]{1,0:T(8,128)S(1)} %get-tuple-element.210, f32[64]{0:T(128)S(1)} %get-tuple-element.182, f32[64]{0:T(128)S(1)} %get-tuple-element.181, s32[1024]{0:T(1024)S(1)} %iota_add_fusion, s32[64]{0:T(128)S(1)} %copy-done), kind=kOutput, calls=%fused_computation.20 | convolution fusion | flops 403046400 | bytes 7344896 | tf_op jit(solution)/shard_map/dot_general | solution.py:42
  47.9 33.8 %all-reduce.5 = bf16[64,3072]{1,0:T(8,128)(2,1)S(1)} all-reduce(f32[64,3072]{1,0:T(8,128)S(1)} %fusion.11), channel_id=1, replica_groups=mesh['dp'=4,'vocab'=8] {'vocab'}, use_global_device_ids=true, to_apply=%region_6.7 | all-reduce | flops 196608 | bytes 1179648 | tf_op jit(solution)/shard_map/psum | solution.py:45
  81.7 0.6 dynamic-slice_convert_fusion
  82.3 4.6 %convert_bitcast_fusion = bf16[3072,1024]{0,1:T(8,128)(2,1)} fusion(bf16[64,3072]{1,0:T(8,128)(2,1)S(1)} %all_gather.21, f32[64,1024]{1,0:T(8,128)S(1)} %get-tuple-element.210, f32[64]{0:T(128)S(1)} %get-tuple-element.182, f32[64]{0:T(128)S(1)} %get-tuple-element.181, s32[1024]{0:T(1024)S(1)} %iota_add_fusion, s32[64]{0:T(128)S(1)} %copy-done), kind=kOutput, calls=%fused_computation.10 | convolution fusion | flops 406192128 | bytes 6951680 | tf_op jit(solution)/shard_map/dot_general | solution.py:38
  86.9 8.6 %copy.6 = bf16[3072,1024]{1,0:T(8,128)(2,1)} copy(bf16[3072,1024]{0,1:T(8,128)(2,1)} %convert_bitcast_fusion) | data formatting | bytes 12582912
  (14 shorter events, 0.2 us)
Async XLA Ops:
  0.6 22.7 %copy-start = (s32[64]{0:T(128)S(1)}, s32[64]{0:T(128)}, u32[]{:S(2)}) copy-start(s32[64]{0:T(128)} %param.7) | copy-start | bytes 772
where the time goes:
time: 97.1 us; the launch traced here: 96.6 us
  blocking collectives  67.4 us (69%)
  matrix products  13.5 us (14%)
  local copies, waits for them, and re-layouts  11.4 us (12%)
  between operations  3.16 us (3%)
  other arithmetic  1.03 us (1%)
    psum x1, blocking collectives, body(): everything = lax.psum(partial_value, 'vocab')  33.8 us
    unnamed x1, blocking collectives  17.2 us
    all_gather x1, blocking collectives, body(): gathered = lax.all_gather(hidden, 'vocab', axis=0, tiled=True)  16.4 us
    unnamed x10, local copies, waits for them, and re-layouts  10.6 us
    dot_general x1, matrix products, body(): lax.dot_general(grad_logits, weight, (((1,), (1,)), ((), ())), preferred_...  4.85 us
    dot_general x1, matrix products, body(): lax.dot_general(gathered, grad_logits, (((0,), (0,)), ((), ())), preferre...  4.58 us
    dot_general x1, matrix products, body(): logits = jnp.dot(gathered, weight, preferred_element_type=jnp.float32)  4.09 us

commit v1 on v0

--- a/solution.py
+++ b/solution.py
@@ -42,7 +42,11 @@
     partial_value = lax.dot_general(
         grad_logits, weight, (((1,), (1,)), ((), ())), preferred_element_type=jnp.float32
     )
-    everything = lax.psum(partial_value, "vocab")
+    everything = partial_value
+    for hop_ in (1, 2, 4):
+        everything = everything + lax.ppermute(
+            everything, "vocab", [(dev, dev ^ hop_) for dev in range(8)]
+        )
     summed = lax.dynamic_slice_in_dim(everything, lax.axis_index("vocab") * own_rows, own_rows, 0)
     return (loss, summed.astype(jnp.bfloat16), d_weight)
 

time: 97.1 us -> 108 us (1.11)
  waiting for transfers between devices: 0 us -> 43.9 us
  blocking collectives: 67.4 us -> 33.6 us
    ppermute x0 -> x3, waiting for transfers between devices: none -> 43.9 us  [body(): lax.ppermute(everything, 'vocab', [(dev, dev ^ hop_) for dev in range(8)])]
    psum x1 -> x0, blocking collectives: 33.8 us -> none  [body(): everything = lax.psum(partial_value, 'vocab')]
  transfers between devices with their start and end apart: 0 -> 3, of which waited for: 0 -> 3; matrix products, arithmetic and copies ran while one was open for 0% -> 13% of each run, Pallas kernels for 0% -> 0%
where the time goes in v1:
time: 108 us; the launch traced here: 107 us
  waiting for transfers between devices  43.9 us (41%)
  blocking collectives  33.6 us (31%)
  matrix products  13.5 us (12%)
  local copies, waits for them, and re-layouts  10.8 us (10%)
  between operations  3.17 us (3%)
  other arithmetic  1.86 us (2%)
    ppermute x3, waiting for transfers between devices, body(): lax.ppermute(everything, 'vocab', [(dev, dev ^ hop_) for dev in range(8)])  43.9 us
    unnamed x1, blocking collectives  17.2 us
    all_gather x1, blocking collectives, body(): gathered = lax.all_gather(hidden, 'vocab', axis=0, tiled=True)  16.4 us
    unnamed x10, local copies, waits for them, and re-layouts  10.5 us
    dot_general x1, matrix products, body(): lax.dot_general(grad_logits, weight, (((1,), (1,)), ((), ())), preferred_...  4.85 us
    dot_general x1, matrix products, body(): lax.dot_general(gathered, grad_logits, (((0,), (0,)), ((), ())), preferre...  4.58 us
    dot_general x1, matrix products, body(): logits = jnp.dot(gathered, weight, preferred_element_type=jnp.float32)  4.09 us
  transfers between devices with their start and end apart: 3, of which 3 were waited for; matrix products, arithmetic and copies ran while one was open for 13% of the time, Pallas kernels for 0%

profile of v1, /device:TPU:0, one launch (start us, length us, event | category | flops | bytes accessed | tf_op | source)
XLA Modules:
  0.0 107.1 jit_solution(15808542395336371869)
XLA Ops:
  0.7 16.4 %all_gather.21 = bf16[64,3072]{1,0:T(8,128)(2,1)S(1)} all-gather(bf16[8,3072]{1,0:T(8,128)(2,1)} %param.5), channel_id=1, replica_groups=mesh['dp'=4,'vocab'=8] {'vocab'}, dimensions={0}, use_global_device_ids=true | all-gather | bytes 442368 | tf_op jit(solution)/shard_map/all_gather | solution.py:24
  17.1 1.2 %dynamic-slice = u32[1]{0:T(128)} dynamic-slice(u32[32]{0:T(128)} %constant.59, u32[]{:T(128)S(6)} %add.88), dynamic_slice_sizes={1} | dynamic-slice | bytes 12
  19.0 4.1 %fusion.15 = (f32[64]{0:T(128)S(1)}, f32[64,1024]{1,0:T(8,128)S(1)}) fusion(bf16[64,3072]{1,0:T(8,128)(2,1)S(1)} %all_gather.21, bf16[3072,1024]{1,0:T(8,128)(2,1)} %param.6), kind=kOutput, calls=%fused_computation.22 | convolution fusion | flops 402718656 | bytes 6947072 | tf_op jit(solution)/shard_map/dot_general | solution.py:25
  23.1 0.2 dynamic-update-slice
  23.3 0.2 fusion.7
  23.6 0.2 dynamic-update-slice.2
  23.8 0.2 dynamic-update-slice.1
  24.0 17.2 %all-reduce.3 = (f32[512]{0:T(512)S(1)}, f32[512]{0:T(512)S(1)}, f32[512]{0:T(512)S(1)}) all-reduce(f32[512]{0:T(512)S(1)} %dynamic-update-slice, f32[512]{0:T(512)S(1)} %dynamic-update-slice.1, f32[512]{0:T(512)S(1)} %dynamic-update-slice.2), channel_id=2, replica_groups=mesh['dp'=4,'vocab'=8] {'vocab'}, use_global_device_ids=true, to_apply=%add | all-reduce | flops 1536 | bytes 12288
  41.2 0.1 reshape.21
  41.3 0.1 reshape.20
  41.4 0.1 reshape.19
  41.4 0.3 while.19
  41.7 4.8 %fusion.12 = f32[64,3072]{1,0:T(8,128)S(1)} fusion(bf16[3072,1024]{1,0:T(8,128)(2,1)} %param.6, f32[64,1024]{1,0:T(8,128)S(1)} %get-tuple-element.210, f32[64]{0:T(128)S(1)} %get-tuple-element.182, f32[64]{0:T(128)S(1)} %get-tuple-element.181, s32[1024]{0:T(1024)S(1)} %iota_add_fusion, s32[64]{0:T(128)S(1)} %copy-done), kind=kOutput, calls=%fused_computation.21 | convolution fusion | flops 403046400 | bytes 7344896 | tf_op jit(solution)/shard_map/dot_general | solution.py:42
  46.7 2.3 %collective-permute-done = f32[64,3072]{1,0:T(8,128)S(1)} collective-permute-done((f32[64,3072]{1,0:T(8,128)S(1)}, f32[64,3072]{1,0:T(8,128)S(1)}, u32[]{:S(2)}, u32[]{:S(2)}) %collective-permute-start) | collective-permute-done | bytes 786464 | tf_op jit(solution)/shard_map/ppermute | solution.py:47
  48.9 0.1 add.84
  49.1 0.1 collective-permute-start.1
  49.1 19.6 %collective-permute-done.1 = f32[64,3072]{1,0:T(8,128)S(1)} collective-permute-done((f32[64,3072]{1,0:T(8,128)S(1)}, f32[64,3072]{1,0:T(8,128)S(1)}, u32[]{:S(2)}, u32[]{:S(2)}) %collective-permute-start.1) | collective-permute-done | bytes 786464 | tf_op jit(solution)/shard_map/ppermute | solution.py:47
  68.7 0.1 add.85
  68.8 0.1 collective-permute-start.2
  68.9 4.6 %convert_bitcast_fusion = bf16[3072,1024]{0,1:T(8,128)(2,1)} fusion(bf16[64,3072]{1,0:T(8,128)(2,1)S(1)} %all_gather.21, f32[64,1024]{1,0:T(8,128)S(1)} %get-tuple-element.210, f32[64]{0:T(128)S(1)} %get-tuple-element.182, f32[64]{0:T(128)S(1)} %get-tuple-element.181, s32[1024]{0:T(1024)S(1)} %iota_add_fusion, s32[64]{0:T(128)S(1)} %copy-done), kind=kOutput, calls=%fused_computation.10 | convolution fusion | flops 406192128 | bytes 6951680 | tf_op jit(solution)/shard_map/dot_general | solution.py:38
  73.5 8.6 %copy.6 = bf16[3072,1024]{1,0:T(8,128)(2,1)} copy(bf16[3072,1024]{0,1:T(8,128)(2,1)} %convert_bitcast_fusion) | data formatting | bytes 12582912
  82.1 0.6 subtract_reduce_fusion
  83.3 22.0 %collective-permute-done.2 = f32[64,3072]{1,0:T(8,128)S(1)} collective-permute-done((f32[64,3072]{1,0:T(8,128)S(1)}, f32[64,3072]{1,0:T(8,128)S(1)}, u32[]{:S(2)}, u32[]{:S(2)}) %collective-permute-start.2) | collective-permute-done | bytes 786464 | tf_op jit(solution)/shard_map/ppermute | solution.py:47
  105.3 0.6 fusion.10
  (17 shorter events, 0.3 us)
Async XLA Ops:
  0.6 22.7 %copy-start = (s32[64]{0:T(128)S(1)}, s32[64]{0:T(128)}, u32[]{:S(2)}) copy-start(s32[64]{0:T(128)} %param.7) | copy-start | bytes 772
  46.6 2.4 %collective-permute-start = (f32[64,3072]{1,0:T(8,128)S(1)}, f32[64,3072]{1,0:T(8,128)S(1)}, u32[]{:S(2)}, u32[]{:S(2)}) collective-permute-start(f32[64,3072]{1,0:T(8,128)S(1)} %fusion.12), channel_id=1, source_target_pairs={{0,1},{1,0},{2,3},{3,2},{4,5},{5,4},{6,7},{7,6},{8,9},{9,8},{10,11... | collective-permute-start | bytes 2359304 | tf_op jit(solution)/shard_map/ppermute | solution.py:47
  49.1 19.6 %collective-permute-start.1 = (f32[64,3072]{1,0:T(8,128)S(1)}, f32[64,3072]{1,0:T(8,128)S(1)}, u32[]{:S(2)}, u32[]{:S(2)}) collective-permute-start(f32[64,3072]{1,0:T(8,128)S(1)} %add.84), channel_id=1, source_target_pairs={{0,2},{1,3},{2,0},{3,1},{4,6},{5,7},{6,4},{7,5},{8,10},{9,11},{10,... | collective-permute-start | bytes 2359304 | tf_op jit(solution)/shard_map/ppermute | solution.py:47
  68.8 36.5 %collective-permute-start.2 = (f32[64,3072]{1,0:T(8,128)S(1)}, f32[64,3072]{1,0:T(8,128)S(1)}, u32[]{:S(2)}, u32[]{:S(2)}) collective-permute-start(f32[64,3072]{1,0:T(8,128)S(1)} %add.85), channel_id=1, source_target_pairs={{0,4},{1,5},{2,6},{3,7},{4,0},{5,1},{6,2},{7,3},{8,12},{9,13},{10,... | collective-permute-start | bytes 2359304 | tf_op jit(solution)/shard_map/ppermute | solution.py:47
